TPU v7x, 256 devices: a whole 4x4x8 slice. The times are simulated.
256 devices in a mesh: px: 32 (over y, z_hi, core), py: 8 (over z_lo, x).
Axes of the slice: x: 4, y: 4, z: 8 (z_hi: 4, z_lo: 2; z = z_hi * 2 + z_lo), core: 2. Of those that a mesh axis runs over, the one named last changes fastest.
Arguments:
- charges_old: float32 [32, 8, 32, 32, 512], P('px', 'py'), may hold values from -0.0026758191 to 0.0026758191
- spline_moduli: float32 [3, 512], replicated, may hold values from 1 to 2.5
Outputs:
- structure: float32 [2, 512, 512, 512], P(None, 'px', 'py')
- energy: float32 [], replicated
- virial: float32 [6], replicated
All inputs are finite; a program needn't handle non-finite values.
Results may differ from a plain program's by a relative error of at most 0.0007.
Values sent between devices are 32-bit elements; how exact they have to be, the bound alone decides.
A program may use at most 128 MiB of HBM per device.

v0:
```python
import functools
import math

import jax
import jax.numpy as jnp
import numpy as np
from jax import lax
from jax.experimental import pallas as pl
from jax.experimental.pallas import tpu as pltpu
from jax.sharding import Mesh
from jax.sharding import PartitionSpec as P

AXES = ("px_0", "px_1", "px_2", "py_0", "py_1")
PX = AXES[:3]
PY = AXES[3:]
MESH = pl.DeviceIdType.MESH
F32 = jnp.float32
BF16 = jnp.bfloat16

beta_nm = 3.12
cell_nm = 0.1
N = 512
HALF = N // 2
NT = (((1,), (1,)), ((), ()))


def split_np(a):
    hi = a.astype(BF16)
    lo = (a - hi.astype(np.float64)).astype(BF16)
    return np.stack([hi, lo])


def angles(rows, cols):
    return 2.0 * math.pi * (np.outer(rows, cols) % N) / N


def z_table():
    z = np.arange(N)
    parts = []
    for b in range(4):
        t = angles(z, 64 * b + np.arange(64))
        parts += [np.cos(t), -np.sin(t)]
    edge = np.zeros((N, 128))
    for b in range(4):
        t = angles(z, np.array([64 * (b + 1)]))[:, 0]
        edge[:, 8 * b] = np.cos(t)
        edge[:, 64 + 8 * b] = -np.sin(t)
    return split_np(np.concatenate(parts + [edge], axis=1))


def y_table():
    r = np.arange(HALF)
    out = []
    for e in range(2):
        t = angles(2 * np.arange(HALF) + e, r)
        out.append(np.concatenate([np.cos(t), np.sin(t)], axis=1))
    return split_np(np.stack(out))


def x_table():
    r = np.arange(HALF)
    out = []
    for a in range(2):
        t = angles(2 * r + a, np.arange(HALF))
        out.append(np.concatenate([np.cos(t), np.sin(t)], axis=1))
    return split_np(np.stack(out))


def split(v):
    hi = v.astype(BF16)
    return hi, (v - hi.astype(F32)).astype(BF16)


def mm(a, b):
    return jnp.dot(a, b, preferred_element_type=F32)


def exchange_kernel(x_ref, wz_ref, wy_ref, r2_ref, zs, r1, zy, send1, recv1, send2, recv2):
    yc, zh, c, lo, xc = [lax.axis_index(a) for a in AXES]
    p = yc * 8 + zh * 2 + c
    me16 = c * 8 + lo * 4 + xc
    me64 = p * 2 + lo
    b = xc + lo * (3 - 2 * xc)

    def peer16(t):
        d = lax.rem(me16 + t, 16)
        dc = lax.div(d, 8)
        dl = lax.rem(lax.div(d, 4), 2)
        dx = lax.rem(d, 4)
        return dc, dl, dx

    def peer64(t):
        d = lax.rem(me64 + t, 64)
        dp = lax.div(d, 2)
        dl = lax.rem(d, 2)
        dx = b + dl * (3 - 2 * b)
        return dp, dl, dx, (lax.div(dp, 8), lax.rem(lax.div(dp, 2), 4), lax.rem(dp, 2), dl, dx)

    barrier = pltpu.get_barrier_semaphore()

    def greet16(t, carry):
        dc, dl, dx = peer16(t)
        pl.semaphore_signal(barrier, inc=1, device_id=(yc, zh, dc, dl, dx), device_id_type=MESH)
        return carry

    def greet64(t, carry):
        pl.semaphore_signal(barrier, inc=1, device_id=peer64(t)[3], device_id_type=MESH)
        return carry

    lax.fori_loop(1, 16, greet16, 0)
    lax.fori_loop(1, 64, greet64, 0)

    def z_step(g, carry):
        rows = x_ref[lax.div(g, 2), :, lax.rem(g, 2)].reshape(256, N)
        hi, low = split(rows)
        out = mm(hi, wz_ref[0]) + mm(low, wz_ref[0]) + mm(hi, wz_ref[1])
        for k in range(4):
            zs[g, k, 0:8] = out[:, 128 * k : 128 * k + 128].reshape(8, 32, 128)
        edge = out[:, 512:640].reshape(8, 32, 128)
        packed = edge[0]
        for r in range(1, 8):
            packed = packed + pltpu.roll(edge[r], r, 1)
        zs[g, 0, 8] = packed
        for k in range(1, 4):
            zs[g, k, 8] = pltpu.roll(packed, 128 - 8 * k, 1)
        return carry

    lax.fori_loop(0, 4, z_step, 0)
    pl.semaphore_wait(barrier, 78)

    def send_y(t, carry):
        dc, dl, dx = peer16(t)
        pltpu.make_async_remote_copy(
            src_ref=zs.at[2 * dc + dl, dx + dl * (3 - 2 * dx)],
            dst_ref=r1.at[:, pl.ds(pl.multiple_of(me16 * 32, 32), 32), :],
            send_sem=send1,
            recv_sem=recv1,
            device_id=(yc, zh, dc, dl, dx),
            device_id_type=MESH,
        ).start()
        return carry

    lax.fori_loop(1, 16, send_y, 0)
    r1[:, pl.ds(pl.multiple_of(me16 * 32, 32), 32), :] = zs[2 * c + lo, b]
    pltpu.make_async_copy(r1.at[:, pl.ds(0, 480), :], r1.at[:, pl.ds(0, 480), :], recv1).wait()

    lane = lax.broadcasted_iota(jnp.int32, (HALF, 128), 1)
    is_edge = (lane == 0) | (lane == 64)
    turn = jnp.where(lane < 64, 1.0, -1.0).astype(F32)

    for e in range(2):

        def fold(i):
            top = r1[i, pl.ds(0, HALF), :]
            bottom = r1[i, pl.ds(HALF, HALF), :]
            return top + bottom if e == 0 else top - bottom

        for r in range(8):
            direct = fold(r)
            edge = fold(8)
            if r:
                edge = pltpu.roll(edge, 128 - r, 1)
            mirror = jnp.where(is_edge, edge, direct)
            plain = jnp.concatenate([direct, mirror], axis=1)
            turned = jnp.concatenate(
                [pltpu.roll(direct, 64, 1) * turn, pltpu.roll(mirror, 64, 1) * turn], axis=1
            )
            hi, low = split(jnp.concatenate([plain, turned], axis=0))
            out = mm(wy_ref[0, e], hi) + mm(wy_ref[1, e], hi) + mm(wy_ref[0, e], low)
            zy[e, pl.ds(r, HALF, stride=8), :] = out[:, :128]
            zy[e, pl.ds(264 * 8 + r, HALF, stride=8), :] = out[:, 128:]
        if e == 0:
            zy[e, pl.ds(520 * 8, 8), :] = zy[e, pl.ds(264 * 8, 8), :]

        def rows_for(dp, dl):
            start = (1 - dl) * (8 * dp) + dl * (264 + 249 - e - 8 * dp)
            return zy.at[e, pl.ds(pl.multiple_of(start * 8, 8), 64), :]

        pltpu.make_async_copy(rows_for(p, lo), r2_ref.at[e, lo, p], recv2.at[e]).start()

        def send_x(t, carry):
            dp, dl, dx, device = peer64(t)
            pltpu.make_async_remote_copy(
                src_ref=rows_for(dp, dl),
                dst_ref=r2_ref.at[e, lo, p],
                send_sem=send2.at[e],
                recv_sem=recv2.at[e],
                device_id=device,
                device_id_type=MESH,
            ).start()
            return carry

        lax.fori_loop(1, 64, send_x, 0)

    pltpu.make_async_copy(r1.at[:, pl.ds(0, 480), :], r1.at[:, pl.ds(0, 480), :], send1).wait()
    for e in range(2):
        sent = zy.at[e, pl.ds(0, 63 * 64), :]
        pltpu.make_async_copy(sent, sent, send2.at[e]).wait()
        pltpu.make_async_copy(r2_ref.at[e], r2_ref.at[e], recv2.at[e]).wait()


def exchange(charges):
    vmem = pl.BlockSpec(memory_space=pltpu.VMEM)
    wz, wy = jnp.asarray(z_table()), jnp.asarray(y_table())
    return pl.pallas_call(
        exchange_kernel,
        out_shape=jax.ShapeDtypeStruct((2, 2, 32, 64, 128), F32),
        in_specs=[vmem] * 3,
        out_specs=pl.BlockSpec(memory_space=pl.ANY),
        scratch_shapes=[
            pltpu.VMEM((4, 4, 9, 32, 128), F32),
            pltpu.VMEM((9, N, 128), F32),
            pltpu.VMEM((2, 528 * 8, 128), F32),
            pltpu.SemaphoreType.DMA,
            pltpu.SemaphoreType.DMA,
            pltpu.SemaphoreType.DMA((2,)),
            pltpu.SemaphoreType.DMA((2,)),
        ],
        compiler_params=pltpu.CompilerParams(
            collective_id=0, has_side_effects=True, vmem_limit_bytes=48 * 2**20
        ),
        name="exchange",
    )(charges.reshape(2, 8, 2, 32, N), wz, wy)


GROUP = 2


def finish_kernel(
    flag_ref, yrow_ref, d_ref, wx_ref, wavex_ref, modx_ref, zcol_ref, out_ref, sums_ref, acc, xz2, modxz
):
    e, step = pl.program_id(0), pl.program_id(1)
    flip = flag_ref[0]

    @pl.when((e == 0) & (step == 0))
    def _():
        acc[...] = jnp.zeros_like(acc)
        mx = wavex_ref[...]
        mz = zcol_ref[:, 0:1]
        xz2[...] = mx * mx + mz * mz
        modxz[...] = modx_ref[...] * zcol_ref[:, 1:2] * (1.0 / (math.pi * (cell_nm * N) ** 3))

    row = lax.broadcasted_iota(jnp.int32, (128, 128), 0)
    col = lax.broadcasted_iota(jnp.int32, (128, 128), 1)
    upper = row >= 64
    within = jnp.where(upper, row - 64, row)
    negated = jnp.where(within == 0, 0, 64 - within)
    target = jnp.where(flip == 1, negated, within) + jnp.where(upper, 64, 0)
    sign = jnp.where((flip == 1) & upper, -1.0, 1.0)
    select = jnp.where(col == target, sign, 0.0).astype(BF16)

    def turned(a):
        his, lows = [], []
        for j in range(GROUP):
            slot = jnp.where(flip == 1, GROUP - 1 - j, j)
            hi, low = split(d_ref[0, a, :, slot].reshape(HALF, 128))
            his.append(lax.dot_general(select, hi, NT, preferred_element_type=F32).astype(BF16))
            lows.append(lax.dot_general(select, low, NT, preferred_element_type=F32).astype(BF16))
        hi, low = jnp.concatenate(his, axis=0), jnp.concatenate(lows, axis=0)
        return mm(hi, wx_ref[0, a]) + mm(low, wx_ref[0, a]) + mm(hi, wx_ref[1, a])

    even, odd = turned(0), turned(1)
    mz = zcol_ref[:, 0:1]
    for j in range(GROUP):

        def parts(v):
            re, im = v[128 * j : 128 * j + 64], v[128 * j + 64 : 128 * j + 128]
            return re[:, :HALF] + im[:, HALF:], im[:, :HALF] - re[:, HALF:]

        er, ei = parts(even)
        orr, oi = parts(odd)
        re = jnp.concatenate([er + orr, er - orr], axis=1)
        im = jnp.concatenate([ei + oi, ei - oi], axis=1)
        out_ref[0, j, 0] = re
        out_ref[1, j, 0] = im
        index = 2 * (GROUP * step + j) + e
        my, mody = yrow_ref[0, index], yrow_ref[1, index]
        msq = xz2[...] + my * my
        anchor = msq == 0.0
        inverse = 1.0 / jnp.where(anchor, 1.0, msq)
        decay = (math.pi**2 / beta_nm**2) * msq
        theta = jnp.where(anchor, 0.0, jnp.exp(-decay) * inverse * modxz[...] * mody)
        power = theta * (re * re + im * im)
        weight = power * (1.0 + decay) * inverse

        def rows(v):
            return jnp.sum(v.reshape(8, 8, N), axis=0)

        wz = weight * mz
        w0, w1, w2 = rows(weight), rows(wz), rows(wz * mz)
        acc[0] += rows(power)
        acc[1] += w0
        acc[2] += w0 * (my * my)
        acc[3] += w2
        acc[4] += w0 * my
        acc[5] += w1
        acc[6] += w1 * my

    @pl.when((e == 1) & (step == pl.num_programs(1) - 1))
    def _():
        mx = wavex_ref[...]

        def lanes(v):
            v = jnp.sum(v, axis=0, keepdims=True)
            return v[:, 0:128] + v[:, 128:256] + v[:, 256:384] + v[:, 384:512]

        sums_ref[...] = jnp.concatenate(
            [
                lanes(acc[0]),
                lanes(acc[1] * (mx * mx)),
                lanes(acc[2]),
                lanes(acc[3]),
                lanes(acc[4] * mx),
                lanes(acc[5] * mx),
                lanes(acc[6]),
                jnp.zeros((1, 128), F32),
            ],
            axis=0,
        )


def finish(gathered, flip, yrow, wavex, modx, zcol):
    wx = jnp.asarray(x_table())
    steps = 8 // GROUP

    def whole(shape):
        return pl.BlockSpec(shape, lambda e, s, flag: (0,) * len(shape))

    return pl.pallas_call(
        finish_kernel,
        out_shape=(
            jax.ShapeDtypeStruct((2, 8, 2, 64, N), F32),
            jax.ShapeDtypeStruct((8, 128), F32),
        ),
        grid_spec=pltpu.PrefetchScalarGridSpec(
            num_scalar_prefetch=1,
            grid=(2, steps),
            in_specs=[
                pl.BlockSpec(memory_space=pltpu.SMEM),
                pl.BlockSpec(
                    (1, 2, 32, GROUP, 8, 128),
                    lambda e, s, flag: (e, 0, 0, s + flag[0] * (steps - 1 - 2 * s), 0, 0),
                ),
                whole((2, 2, HALF, N)),
                whole((1, N)),
                whole((1, N)),
                whole((64, 128)),
            ],
            out_specs=[
                pl.BlockSpec((2, GROUP, 1, 64, N), lambda e, s, flag: (0, s, e, 0, 0)),
                whole((8, 128)),
            ],
            scratch_shapes=[
                pltpu.VMEM((7, 8, N), F32),
                pltpu.VMEM((64, N), F32),
                pltpu.VMEM((64, N), F32),
            ],
        ),
        compiler_params=pltpu.CompilerParams(vmem_limit_bytes=40 * 2**20),
        name="finish",
    )(flip, yrow, gathered, wx, wavex, modx, zcol)


def signed_wave(mode_index):
    shifted = mode_index - N * (mode_index >= HALF).astype(jnp.int32)
    return shifted.astype(F32) / (cell_nm * N)


def body(charges_old, spline_moduli):
    row = lax.axis_index(PX)
    col = lax.axis_index(PY)
    lo = lax.axis_index("py_0")
    ky = row * 16 + jnp.arange(16, dtype=jnp.int32)
    kz = col * 64 + jnp.arange(64, dtype=jnp.int32)
    kx = jnp.arange(N, dtype=jnp.int32)
    mody = lax.dynamic_slice_in_dim(spline_moduli[1], row * 16, 16)
    modz = lax.dynamic_slice_in_dim(spline_moduli[2], col * 64, 64)
    yrow = jnp.stack([signed_wave(ky), mody])
    pick = jnp.arange(128, dtype=jnp.int32)[None, :]
    zcol = jnp.where(pick == 0, signed_wave(kz)[:, None], modz[:, None])
    wavex = signed_wave(kx)[None, :]
    modx = spline_moduli[0][None, :]

    gathered = exchange(charges_old).reshape(2, 2, 32, 8, 8, 128)
    structure, sums = finish(gathered, lo.astype(jnp.int32).reshape(1), yrow, wavex, modx, zcol)
    totals = lax.psum(jnp.sum(sums, axis=1), AXES)
    energy = 0.5 * totals[0]
    virial = energy * jnp.array([1.0, 1.0, 1.0, 0.0, 0.0, 0.0], dtype=F32) - totals[1:7]
    return structure.reshape(2, 16, 64, N), energy, virial


def solution(mesh):
    torus = Mesh(mesh.devices.reshape(4, 4, 2, 2, 4), AXES)
    return jax.shard_map(
        body,
        mesh=torus,
        in_specs=(P(PX, PY, None, None, None), P()),
        out_specs=(P(None, PX, PY, None), P(), P()),
        check_vma=False,
    )
```

profile of v0, /device:TPU:1, one launch (start us, length us, event | category | flops | bytes accessed | tf_op | source)
XLA Modules:
  0.0 236.2 jit_solution(17292893403452241756)
XLA Ops:
  0.7 0.8 fusion.9
  1.5 0.1 dynamic-slice_bitcast_fusion
  1.6 0.1 fusion.8
  1.7 0.1 broadcast_select_fusion.zcol_ref
  1.7 0.0 copy-start.1
  1.8 1.2 copy-done.1
  3.0 0.0 copy-start.2
  3.0 1.6 copy-done.2
  4.6 0.0 copy-start.3
  4.6 1.3 copy-done.3
  5.9 142.0 %exchange.1 = f32[2,2,32,64,128]{4,3,2,1,0:T(8,128)} custom-call(f32[2,8,2,32,512]{4,3,2,1,0:T(8,128)S(1)} %bitcast.9, bf16[2,512,640]{2,1,0:T(8,128)(2,1)S(1)} %copy-done.3, bf16[2,2,256,512]{3,2,1,0:T(8,128)(2,1)S(1)} %copy-done.1), custom_call_target="tpu_custom_call" | custom-call | tf_op jit(solution)/shard_map/exchange/pallas_call | solution.py:205
  147.9 0.0 copy-start.4
  147.9 0.0 copy-start
  147.9 2.2 copy-done
  150.1 9.6 %finish.1 = (f32[2,8,2,64,512]{4,3,2,1,0:T(8,128)}, f32[8,128]{1,0:T(8,128)S(1)}) custom-call(s32[1]{0:T(128)} %bitcast.flag_ref, f32[2,16]{1,0:T(2,128)S(1)} %pad_maximum_fusion.yrow_ref, f32[2,2,32,8,8,128]{5,4,3,2,1,0:T(8,128)S(1)} %bitcast.8, bf16[2,2,256,512]{3,2,1,0:T(8,128)(2,1)S(1)} %copy-done.1, f32[1,512]{1,0:T(1,128)S(1)} %fusion.2.wavex_ref, ...), custom_call_target="tpu_custom_call" | custom-call | tf_op jit(solution)/shard_map/finish/pallas_call | solution.py:329
  159.7 0.1 reduce_sum.9
  159.8 74.6 %psum.7 = f32[8]{0:T(128)S(1)} all-reduce(f32[8]{0:T(128)S(1)} %reduce_sum.9), channel_id=1, replica_groups=mesh['px_0'=4,'px_1'=4,'px_2'=2,'py_0'=2,'py_1'=4] {'px_0','px_1','px_2'..., use_global_device_ids=true, to_apply=%region_1.2 | all-reduce | flops 8 | bytes 64 | tf_op jit(solution)/shard_map/psum | solution.py:386
  234.5 0.0 copy-done.4
  234.5 0.6 slice_subtract_fusion
  (4 shorter events, 0.0 us)
Async XLA Ops:
  1.7 1.2 copy-start.1
  3.0 1.6 copy-start.2
  4.6 1.3 copy-start.3
  147.9 86.6 %copy-start.4 = (f32[6]{0:T(128)S(1)}, f32[6]{0:T(128)}, u32[]{:S(2)}) copy-start(f32[6]{0:T(128)} %constant.67.clone) | copy-start | bytes 76
  147.9 2.2 copy-start
where the time goes:
time: 237 us; the launch traced here: 236 us
  Pallas kernels  152 us (64%)
  blocking collectives  74.6 us (31%)
  local copies, waits for them, and re-layouts  7.21 us (3%)
    pallas_call x1, Pallas kernels, exchange(): pl.pallas_call(exchange_kernel, out_shape=jax.ShapeDtypeStruct((2, 2, 32,...  142 us
    psum x1, blocking collectives, body(): totals = lax.psum(jnp.sum(sums, axis=1), AXES)  74.6 us
    pallas_call x1, Pallas kernels, finish(): pl.pallas_call(finish_kernel, out_shape=(jax.ShapeDtypeStruct((2, 8, 2, 6...  9.59 us
    unnamed x10, local copies, waits for them, and re-layouts  6.32 us

commit v1 on v0

--- a/solution.py
+++ b/solution.py
@@ -75,7 +75,15 @@
     return jnp.dot(a, b, preferred_element_type=F32)
 
 
-def exchange_kernel(x_ref, wz_ref, wy_ref, r2_ref, zs, r1, zy, send1, recv1, send2, recv2):
+def exchange_kernel(
+    x_hbm, wz_hbm, wy_hbm, r2_ref, x_ref, wz_ref, wy_ref, zs, r1, zy, load, send1, recv1, send2, recv2
+):
+    loads = [
+        pltpu.make_async_copy(source, target, load.at[i])
+        for i, (source, target) in enumerate(((x_hbm, x_ref), (wz_hbm, wz_ref), (wy_hbm, wy_ref)))
+    ]
+    for copy in loads:
+        copy.start()
     yc, zh, c, lo, xc = [lax.axis_index(a) for a in AXES]
     p = yc * 8 + zh * 2 + c
     me16 = c * 8 + lo * 4 + xc
@@ -125,6 +133,8 @@
             zs[g, k, 8] = pltpu.roll(packed, 128 - 8 * k, 1)
         return carry
 
+    loads[0].wait()
+    loads[1].wait()
     lax.fori_loop(0, 4, z_step, 0)
     pl.semaphore_wait(barrier, 78)
 
@@ -144,6 +154,7 @@
     r1[:, pl.ds(pl.multiple_of(me16 * 32, 32), 32), :] = zs[2 * c + lo, b]
     pltpu.make_async_copy(r1.at[:, pl.ds(0, 480), :], r1.at[:, pl.ds(0, 480), :], recv1).wait()
 
+    loads[2].wait()
     lane = lax.broadcasted_iota(jnp.int32, (HALF, 128), 1)
     is_edge = (lane == 0) | (lane == 64)
     turn = jnp.where(lane < 64, 1.0, -1.0).astype(F32)
@@ -200,24 +211,27 @@
 
 
 def exchange(charges):
-    vmem = pl.BlockSpec(memory_space=pltpu.VMEM)
     wz, wy = jnp.asarray(z_table()), jnp.asarray(y_table())
     return pl.pallas_call(
         exchange_kernel,
         out_shape=jax.ShapeDtypeStruct((2, 2, 32, 64, 128), F32),
-        in_specs=[vmem] * 3,
+        in_specs=[pl.BlockSpec(memory_space=pl.ANY)] * 3,
         out_specs=pl.BlockSpec(memory_space=pl.ANY),
         scratch_shapes=[
+            pltpu.VMEM((2, 8, 2, 32, N), F32),
+            pltpu.VMEM((2, N, 640), BF16),
+            pltpu.VMEM((2, 2, HALF, N), BF16),
             pltpu.VMEM((4, 4, 9, 32, 128), F32),
             pltpu.VMEM((9, N, 128), F32),
             pltpu.VMEM((2, 528 * 8, 128), F32),
+            pltpu.SemaphoreType.DMA((3,)),
             pltpu.SemaphoreType.DMA,
             pltpu.SemaphoreType.DMA,
             pltpu.SemaphoreType.DMA((2,)),
             pltpu.SemaphoreType.DMA((2,)),
         ],
         compiler_params=pltpu.CompilerParams(
-            collective_id=0, has_side_effects=True, vmem_limit_bytes=48 * 2**20
+            collective_id=0, has_side_effects=True, vmem_limit_bytes=62 * 2**20
         ),
         name="exchange",
     )(charges.reshape(2, 8, 2, 32, N), wz, wy)
@@ -226,19 +240,25 @@
 GROUP = 2
 
 
-def finish_kernel(
-    flag_ref, yrow_ref, d_ref, wx_ref, wavex_ref, modx_ref, zcol_ref, out_ref, sums_ref, acc, xz2, modxz
-):
+def signed_wave(mode_index):
+    shifted = mode_index - N * (mode_index >= HALF).astype(jnp.int32)
+    return shifted.astype(F32) / (cell_nm * N)
+
+
+def finish_kernel(place_ref, mod_smem, d_ref, wx_ref, mod_ref, out_ref, sums_ref, acc, xz2, modxz):
     e, step = pl.program_id(0), pl.program_id(1)
-    flip = flag_ref[0]
+    flip, px, py = place_ref[0], place_ref[1], place_ref[2]
+    mx = signed_wave(lax.broadcasted_iota(jnp.int32, (1, N), 1))
+    mz = signed_wave(64 * py + lax.broadcasted_iota(jnp.int32, (64, 1), 0))
 
     @pl.when((e == 0) & (step == 0))
     def _():
         acc[...] = jnp.zeros_like(acc)
-        mx = wavex_ref[...]
-        mz = zcol_ref[:, 0:1]
         xz2[...] = mx * mx + mz * mz
-        modxz[...] = modx_ref[...] * zcol_ref[:, 1:2] * (1.0 / (math.pi * (cell_nm * N) ** 3))
+        modz = pltpu.roll(jnp.broadcast_to(mod_ref[2:3, :], (8, N)), lax.rem(N - 64 * py, N), 1)
+        modz = jnp.broadcast_to(modz[0:1, :128], (128, 128)).T[:64]
+        modz = jnp.concatenate([modz] * 4, axis=1)
+        modxz[...] = mod_ref[0:1, :] * modz * (1.0 / (math.pi * (cell_nm * N) ** 3))
 
     row = lax.broadcasted_iota(jnp.int32, (128, 128), 0)
     col = lax.broadcasted_iota(jnp.int32, (128, 128), 1)
@@ -260,7 +280,6 @@
         return mm(hi, wx_ref[0, a]) + mm(low, wx_ref[0, a]) + mm(hi, wx_ref[1, a])
 
     even, odd = turned(0), turned(1)
-    mz = zcol_ref[:, 0:1]
     for j in range(GROUP):
 
         def parts(v):
@@ -273,8 +292,9 @@
         im = jnp.concatenate([ei + oi, ei - oi], axis=1)
         out_ref[0, j, 0] = re
         out_ref[1, j, 0] = im
-        index = 2 * (GROUP * step + j) + e
-        my, mody = yrow_ref[0, index], yrow_ref[1, index]
+        ky = 16 * px + 2 * (GROUP * step + j) + e
+        my = (ky - jnp.where(ky >= HALF, N, 0)).astype(F32) * (1.0 / (cell_nm * N))
+        mody = mod_smem[1, ky]
         msq = xz2[...] + my * my
         anchor = msq == 0.0
         inverse = 1.0 / jnp.where(anchor, 1.0, msq)
@@ -298,8 +318,6 @@
 
     @pl.when((e == 1) & (step == pl.num_programs(1) - 1))
     def _():
-        mx = wavex_ref[...]
-
         def lanes(v):
             v = jnp.sum(v, axis=0, keepdims=True)
             return v[:, 0:128] + v[:, 128:256] + v[:, 256:384] + v[:, 384:512]
@@ -319,7 +337,7 @@
         )
 
 
-def finish(gathered, flip, yrow, wavex, modx, zcol):
+def finish(gathered, place, moduli):
     wx = jnp.asarray(x_table())
     steps = 8 // GROUP
 
@@ -342,9 +360,7 @@
                     lambda e, s, flag: (e, 0, 0, s + flag[0] * (steps - 1 - 2 * s), 0, 0),
                 ),
                 whole((2, 2, HALF, N)),
-                whole((1, N)),
-                whole((1, N)),
-                whole((64, 128)),
+                whole((3, N)),
             ],
             out_specs=[
                 pl.BlockSpec((2, GROUP, 1, 64, N), lambda e, s, flag: (0, s, e, 0, 0)),
@@ -356,34 +372,86 @@
                 pltpu.VMEM((64, N), F32),
             ],
         ),
-        compiler_params=pltpu.CompilerParams(vmem_limit_bytes=40 * 2**20),
+        compiler_params=pltpu.CompilerParams(vmem_limit_bytes=62 * 2**20),
         name="finish",
-    )(flip, yrow, gathered, wx, wavex, modx, zcol)
-
-
-def signed_wave(mode_index):
-    shifted = mode_index - N * (mode_index >= HALF).astype(jnp.int32)
-    return shifted.astype(F32) / (cell_nm * N)
+    )(place, moduli, gathered, wx, moduli)
+
+
+def total_kernel(part_ref, out_ref, first, second, middle, send, recv):
+    yc, zh, c, lo, xc = [lax.axis_index(a) for a in AXES]
+    inner = c * 8 + lo * 4 + xc
+    outer = yc * 4 + zh
+
+    def device(stage, t):
+        if stage == 0:
+            d = lax.rem(inner + t, 16)
+            return yc, zh, lax.div(d, 8), lax.rem(lax.div(d, 4), 2), lax.rem(d, 4)
+        d = lax.rem(outer + t, 16)
+        return lax.div(d, 4), lax.rem(d, 4), c, lo, xc
+
+    barrier = pltpu.get_barrier_semaphore()
+    for stage in range(2):
+
+        def greet(t, carry):
+            pl.semaphore_signal(
+                barrier, inc=1, device_id=device(stage, t), device_id_type=MESH
+            )
+            return carry
+
+        lax.fori_loop(1, 16, greet, 0)
+    pl.semaphore_wait(barrier, 30)
+
+    def exchange_all(stage, source, slots, me):
+        slots[me] = source[...]
+
+        def put(t, carry):
+            pltpu.make_async_remote_copy(
+                src_ref=source,
+                dst_ref=slots.at[me],
+                send_sem=send.at[stage],
+                recv_sem=recv.at[stage],
+                device_id=device(stage, t),
+                device_id_type=MESH,
+            ).start()
+            return carry
+
+        lax.fori_loop(1, 16, put, 0)
+        many = slots.at[pl.ds(0, 15)]
+        pltpu.make_async_copy(many, many, recv.at[stage]).wait()
+        return jnp.sum(slots[...], axis=0)
+
+    middle[...] = exchange_all(0, part_ref, first, inner)
+    out_ref[...] = jnp.broadcast_to(
+        jnp.sum(exchange_all(1, middle, second, outer), axis=1, keepdims=True), (8, 128)
+    )
+    for stage in range(2):
+        many = first.at[pl.ds(0, 15)]
+        pltpu.make_async_copy(many, many, send.at[stage]).wait()
+
+
+def total(parts):
+    return pl.pallas_call(
+        total_kernel,
+        out_shape=jax.ShapeDtypeStruct((8, 128), F32),
+        in_specs=[pl.BlockSpec(memory_space=pltpu.VMEM)],
+        out_specs=pl.BlockSpec(memory_space=pltpu.VMEM),
+        scratch_shapes=[
+            pltpu.VMEM((16, 8, 128), F32),
+            pltpu.VMEM((16, 8, 128), F32),
+            pltpu.VMEM((8, 128), F32),
+            pltpu.SemaphoreType.DMA((2,)),
+            pltpu.SemaphoreType.DMA((2,)),
+        ],
+        compiler_params=pltpu.CompilerParams(collective_id=1, has_side_effects=True),
+        name="total",
+    )(parts)
 
 
 def body(charges_old, spline_moduli):
-    row = lax.axis_index(PX)
-    col = lax.axis_index(PY)
-    lo = lax.axis_index("py_0")
-    ky = row * 16 + jnp.arange(16, dtype=jnp.int32)
-    kz = col * 64 + jnp.arange(64, dtype=jnp.int32)
-    kx = jnp.arange(N, dtype=jnp.int32)
-    mody = lax.dynamic_slice_in_dim(spline_moduli[1], row * 16, 16)
-    modz = lax.dynamic_slice_in_dim(spline_moduli[2], col * 64, 64)
-    yrow = jnp.stack([signed_wave(ky), mody])
-    pick = jnp.arange(128, dtype=jnp.int32)[None, :]
-    zcol = jnp.where(pick == 0, signed_wave(kz)[:, None], modz[:, None])
-    wavex = signed_wave(kx)[None, :]
-    modx = spline_moduli[0][None, :]
-
+    place = jnp.stack([lax.axis_index("py_0"), lax.axis_index(PX), lax.axis_index(PY)])
     gathered = exchange(charges_old).reshape(2, 2, 32, 8, 8, 128)
-    structure, sums = finish(gathered, lo.astype(jnp.int32).reshape(1), yrow, wavex, modx, zcol)
-    totals = lax.psum(jnp.sum(sums, axis=1), AXES)
+    structure, sums = finish(gathered, place.astype(jnp.int32), spline_moduli)
+    totals = total(sums)[:, 0]
     energy = 0.5 * totals[0]
     virial = energy * jnp.array([1.0, 1.0, 1.0, 0.0, 0.0, 0.0], dtype=F32) - totals[1:7]
     return structure.reshape(2, 16, 64, N), energy, virial

time: 237 us -> 174 us (0.73)
  blocking collectives: 74.6 us -> 0 us
  Pallas kernels: 152 us -> 168 us
  local copies, waits for them, and re-layouts: 7.21 us -> 2 us
    psum x1 -> x0, blocking collectives: 74.6 us -> none  [body(): totals = lax.psum(jnp.sum(sums, axis=1), AXES)]
    pallas_call x0 -> x1, Pallas kernels: none -> 14 us  [total(): pl.pallas_call(total_kernel, out_shape=jax.ShapeDtypeStruct((8, 128), F32...]
    unnamed x10 -> x2, local copies, waits for them, and re-layouts: 6.32 us -> 0.01 us
where the time goes in v1:
time: 174 us
  Pallas kernels  168 us (97%)
  between operations  2.45 us (1%)
  local copies, waits for them, and re-layouts  2 us (1%)
    pallas_call x1, Pallas kernels, exchange(): pl.pallas_call(exchange_kernel, out_shape=jax.ShapeDtypeStruct((2, 2, 32,...  142 us
    pallas_call x1, Pallas kernels, total(): pl.pallas_call(total_kernel, out_shape=jax.ShapeDtypeStruct((8, 128), F32...  14 us
    pallas_call x1, Pallas kernels, finish(): pl.pallas_call(finish_kernel, out_shape=(jax.ShapeDtypeStruct((2, 8, 2, 6...  11.8 us

profile of v1, /device:TPU:1, one launch (start us, length us, event | category | flops | bytes accessed | tf_op | source)
XLA Modules:
  0.0 173.6 jit_solution(11991255991219025697)
XLA Ops:
  0.6 0.6 pad_add_fusion.place_ref
  1.3 142.2 %exchange.1 = f32[2,2,32,64,128]{4,3,2,1,0:T(8,128)} custom-call(f32[2,8,2,32,512]{4,3,2,1,0:T(8,128)} %bitcast.8, bf16[2,512,640]{2,1,0:T(8,128)(2,1)} %constant.35.clone.wz_hbm, bf16[2,2,256,512]{3,2,1,0:T(8,128)(2,1)} %constant.36.clone.wy_hbm.wx_ref), custom_call_target="tpu_custom_call" | custom-call | tf_op jit(solution)/shard_map/exchange/pallas_call | solution.py:215
  143.4 0.0 copy-start
  143.5 11.8 %finish.1 = (f32[2,8,2,64,512]{4,3,2,1,0:T(8,128)}, f32[8,128]{1,0:T(8,128)}) custom-call(s32[3]{0:T(128)} %pad_add_fusion.place_ref, f32[3,512]{1,0:T(4,128)} %mod_ref.1, f32[2,2,32,8,8,128]{5,4,3,2,1,0:T(8,128)} %bitcast.7, bf16[2,2,256,512]{3,2,1,0:T(8,128)(2,1)} %constant.36.clone.wy_hbm.wx_ref, f32[3,512]{1,0:T(4,128)} %mod_ref.1), custom_call_target="tpu_custom_call" | custom-call | tf_op jit(solution)/shard_map/finish/pallas_call | solution.py:347
  155.3 14.0 %total.1 = f32[8,128]{1,0:T(8,128)} custom-call(f32[8,128]{1,0:T(8,128)} %get-tuple-element.6.part_ref), custom_call_target="tpu_custom_call" | custom-call | tf_op jit(solution)/shard_map/total/pallas_call | solution.py:433
  169.3 1.2 slice.13
  171.1 0.8 slice_reduce_fusion
  171.9 0.0 copy-done
  171.9 0.5 multiply_subtract_fusion
Async XLA Ops:
  143.4 28.5 %copy-start = (f32[6]{0:T(128)S(1)}, f32[6]{0:T(128)}, u32[]{:S(2)}) copy-start(f32[6]{0:T(128)} %constant.37.clone) | copy-start | bytes 76
